TPU v7x, 32 devices: a whole 2x2x4 slice. The times are simulated.
32 devices in a mesh: depth: 16 (over z, y, x), spec: 2 (over core).
Axes of the slice: x: 2, y: 2, z: 4, core: 2. Of those that a mesh axis runs over, the one named last changes fastest.
Arguments:
- emission: bfloat16 [512, 64, 2048], P('depth', 'spec'), may hold values from 0.099609375 to 2
- opacity: bfloat16 [512, 64, 2048], P('depth', 'spec'), may hold values from 0.29882812 to 3
- bin_extinction: float32 [64], P('spec'), may hold values from 0.1 to 30
- entry: int32 [2048], replicated, may hold values from 0 to 127
- exit_cell: int32 [2048], replicated, may hold values from 384 to 512
- response: float32 [3, 64], P(None, 'spec'), may hold values from 0.05 to 1
Outputs:
- nearer_slab_rgb: float32 [16, 3, 2048], P('depth')
- image: float32 [3, 2048], replicated
All inputs are finite; a program needn't handle non-finite values.
Results may differ from a plain program's by a relative error of at most 0.0003.
Values sent between devices are 32-bit elements; how exact they have to be, the bound alone decides.
A program may use at most 64 MiB of HBM per device.

v0:
```python
import jax
import jax.numpy as jnp
from jax import lax
from jax.sharding import PartitionSpec as P


def merge_slabs(earlier, later):
    return (earlier[0] + earlier[1] * later[0], earlier[1] * later[1])


def body(emission, opacity, bin_extinction, entry, exit_cell, response):
    cells = emission.shape[0]
    sections = lax.axis_size("depth")
    cell_step = 1.0 / (cells * sections)
    depth = lax.axis_index("depth") * cells + jnp.arange(cells, dtype=jnp.int32)
    inside = (depth[:, None] >= entry[None, :]) & (depth[:, None] < exit_cell[None, :])
    live = jnp.where(inside, 1.0, 0.0).astype(jnp.float32)
    tau = bin_extinction[None, :, None] * opacity.astype(jnp.float32) * live[:, None, :] * cell_step
    rows = jnp.arange(cells, dtype=jnp.int32)
    lower = jnp.where(rows[None, :] < rows[:, None], 1.0, 0.0).astype(jnp.float32)
    before = jnp.einsum("ij,jbr->ibr", lower, tau, precision=lax.Precision.HIGHEST)
    light = jnp.sum(
        emission.astype(jnp.float32) * live[:, None, :] * cell_step * jnp.exp(-before), axis=0
    )
    trans = jnp.exp(-jnp.sum(tau, axis=0))
    pieces = (
        lax.all_to_all(light[None], "depth", split_axis=2, concat_axis=0, tiled=True),
        lax.all_to_all(trans[None], "depth", split_axis=2, concat_axis=0, tiled=True),
    )
    totals = lax.associative_scan(merge_slabs, (pieces[0], pieces[1]), axis=0)
    lead_light = jnp.concatenate([jnp.zeros_like(pieces[0][:1]), totals[0][:-1]], axis=0)
    lead_trans = jnp.concatenate([jnp.ones_like(pieces[1][:1]), totals[1][:-1]], axis=0)
    moved_light = lax.all_to_all(lead_light, "depth", split_axis=0, concat_axis=2, tiled=True)
    moved_trans = lax.all_to_all(lead_trans, "depth", split_axis=0, concat_axis=2, tiled=True)
    nearer_radiance = moved_light[0]
    nearer_transparency = moved_trans[0]
    front_part = jnp.dot(response, nearer_radiance, precision=lax.Precision.HIGHEST)
    slab_portion = jnp.dot(response, nearer_transparency * light, precision=lax.Precision.HIGHEST)
    nearer_slab_rgb, slab_colour_rgb = lax.psum((front_part, slab_portion), "spec")
    image = lax.psum(slab_colour_rgb, "depth")
    return (nearer_slab_rgb[None], image)


def solution(mesh):
    placed = (
        P("depth", "spec", None),
        P("depth", "spec", None),
        P("spec"),
        P(),
        P(),
        P(None, "spec"),
    )
    return jax.shard_map(
        body, mesh=mesh, in_specs=placed, out_specs=(P("depth", None, None), P()), check_vma=False
    )
```

profile of v0, /device:TPU:0, one launch (start us, length us, event | category | flops | bytes accessed | tf_op | source)
XLA Modules:
  0.0 190.8 jit_solution(17573433646198136472)
XLA Ops:
  0.7 0.8 and_select_fusion
  1.5 5.9 %fusion = f32[32,2048]{1,0:T(8,128)S(1)} fusion(f32[32]{0:T(128)} %param.8, f32[32,2048]{1,0:T(8,128)S(1)} %and_select_fusion, bf16[32,32,2048]{2,1,0:T(8,128)(2,1)} %param.7), kind=kLoop, calls=%fused_computation.2 | loop fusion | flops 10420224 | bytes 4718720 | tf_op jit(solution)/shard_map/reduce_sum | solution.py:25
  7.4 0.6 copy.48
  8.0 0.5 broadcast.88
  8.5 9.3 %reduce = f32[2048,32]{1,0:T(8,128)S(1)} reduce(f32[2048,1,32]{2,1,0:T(1,128)S(1)} %bitcast.63, f32[]{:T(128)} %broadcast.88), dimensions={1}, to_apply=%bitcast.47.reduce_sub_computation | reduce | bytes 524292
  17.9 1.1 reshape.76
  19.0 8.3 %all-to-all-start.1 = ((f32[16,1,4096]{2,1,0:T(1,128)}), f32[16,1,4096]{2,1,0:T(1,128)S(1)}, u32[]{:S(2)}, u32[]{:S(2)}) async-start(f32[16,1,4096]{2,1,0:T(1,128)} %reshape.76), calls=%async_computation.1 | async-start | bytes 524288 | tf_op jit(solution)/shard_map/all_to_all | solution.py:28
  27.4 21.2 %multiply_reduce_fusion = f32[32,2048]{1,0:T(8,128)S(1)} fusion(bf16[32,32,2048]{2,1,0:T(8,128)(2,1)} %param.6, f32[32]{0:T(128)S(1)} %copy-done.1, f32[32,2048]{1,0:T(8,128)S(1)} %and_select_fusion, bf16[32,32,2048]{2,1,0:T(8,128)(2,1)} %param.7), kind=kOutput, calls=%fused_computation | convolution fusion | flops 826214400 | bytes 8913024 | tf_op jit(solution)/shard_map/ij,jbr->ibr/dot_general | solution.py:21
  48.6 0.6 copy.46
  49.2 9.6 %reduce.2 = f32[2048,32]{1,0:T(8,128)S(1)} reduce(f32[2048,1,32]{2,1,0:T(1,128)S(1)} %bitcast.66, f32[]{:T(128)} %broadcast.88), dimensions={1}, to_apply=%bitcast.45.reduce_sub_computation | reduce | bytes 524292
  58.8 1.2 reshape.74
  59.9 6.9 %all-to-all-start = ((f32[16,1,4096]{2,1,0:T(1,128)}), f32[16,1,4096]{2,1,0:T(1,128)S(1)}, u32[]{:S(2)}, u32[]{:S(2)}) async-start(f32[16,1,4096]{2,1,0:T(1,128)} %reshape.74), calls=%async_computation | async-start | bytes 524288 | tf_op jit(solution)/shard_map/all_to_all | solution.py:27
  66.8 1.3 reduce.1
  68.1 1.8 reshape.77
  69.9 0.6 copy.49
  70.9 5.3 %all-to-all-done = f32[16,1,4096]{2,1,0:T(1,128)S(1)} async-done(((f32[16,1,4096]{2,1,0:T(1,128)}), f32[16,1,4096]{2,1,0:T(1,128)S(1)}, u32[]{:S(2)}, u32[]{:S(2)}) %all-to-all-start) | async-done | bytes 262176 | tf_op jit(solution)/shard_map/all_to_all | solution.py:27
  76.2 1.3 reduce.3
  77.4 1.8 reshape.75
  79.3 0.3 copy.57
  80.7 0.1 slice.138
  80.8 0.1 slice.135
  80.9 0.1 slice.133
  81.0 0.1 slice.136
  81.5 0.4 pad.59
  81.9 0.4 pad.58
  82.4 0.4 pad.56
  82.8 0.4 pad.57
  83.4 0.2 pad.60
  83.7 0.2 pad.62
  83.9 0.2 pad.63
  84.1 0.2 pad.61
  84.5 0.2 pad.84
  84.8 0.2 pad.125
  85.2 0.7 concatenate.31.clone
  85.9 3.5 %all-to-all-start.3 = ((f32[16,32,128]{2,1,0:T(8,128)}), f32[16,32,128]{2,1,0:T(8,128)S(1)}, u32[]{:S(2)}, u32[]{:S(2)}) async-start(f32[16,32,128]{2,1,0:T(8,128)} %concatenate.31.clone), calls=%async_computation.3 | async-start | bytes 524288 | tf_op jit(solution)/shard_map/all_to_all | solution.py:34
  89.5 0.2 pad.82
  89.7 0.2 pad.124
  90.1 0.7 concatenate.29.clone
  90.8 7.8 %all-to-all-done.3 = f32[16,32,128]{2,1,0:T(8,128)S(1)} async-done(((f32[16,32,128]{2,1,0:T(8,128)}), f32[16,32,128]{2,1,0:T(8,128)S(1)}, u32[]{:S(2)}, u32[]{:S(2)}) %all-to-all-start.3) | async-done | bytes 262176 | tf_op jit(solution)/shard_map/all_to_all | solution.py:34
  98.7 3.5 %all-to-all-start.2 = ((f32[16,32,128]{2,1,0:T(8,128)}), f32[16,32,128]{2,1,0:T(8,128)S(1)}, u32[]{:S(2)}, u32[]{:S(2)}) async-start(f32[16,32,128]{2,1,0:T(8,128)} %concatenate.29.clone), calls=%async_computation.2 | async-start | bytes 524288 | tf_op jit(solution)/shard_map/all_to_all | solution.py:33
  102.2 0.2 copy.55
  102.4 9.0 %all-to-all-done.2 = f32[16,32,128]{2,1,0:T(8,128)S(1)} async-done(((f32[16,32,128]{2,1,0:T(8,128)}), f32[16,32,128]{2,1,0:T(8,128)S(1)}, u32[]{:S(2)}, u32[]{:S(2)}) %all-to-all-start.2) | async-done | bytes 262176 | tf_op jit(solution)/shard_map/all_to_all | solution.py:33
  111.4 0.2 copy.52
  111.5 0.3 convolution_bitcast_fusion
  111.9 0.3 convolution_bitcast_fusion.1
  112.2 3.6 %all-reduce.18 = (f32[1,3,2048]{2,1,0:T(4,128)S(1)}, f32[3,2048]{1,0:T(4,128)S(1)}) all-reduce(f32[1,3,2048]{2,1,0:T(4,128)S(1)} %convolution_bitcast_fusion.1, f32[3,2048]{1,0:T(4,128)S(1)} %convolution_bitcast_fusion), channel_id=1, replica_groups=mesh['depth'=16,'spec'=2] {'spec'}, use_global_device_ids=true, to_apply=%region_2.3 | all-reduce | flops 12288 | bytes 98304 | tf_op jit(solution)/shard_map/psum | solution.py:39
  115.8 0.6 copy.56
  116.5 74.4 %psum.23 = f32[3,2048]{1,0:T(4,128)} all-reduce(f32[3,2048]{1,0:T(4,128)S(1)} %get-tuple-element.13), channel_id=1, replica_groups=mesh['depth'=16,'spec'=2] {'depth'}, use_global_device_ids=true, to_apply=%region_4.5 | all-reduce | flops 6144 | bytes 49152 | tf_op jit(solution)/shard_map/psum | solution.py:40
  (45 shorter events, 2.2 us)
Async XLA Ops:
  0.6 110.9 %copy-start = (f32[3,32]{1,0:T(4,128)S(1)}, f32[3,32]{1,0:T(4,128)}, u32[]{:S(2)}) copy-start(f32[3,32]{1,0:T(4,128)} %param.11) | copy-start | bytes 1156
  1.5 25.9 %copy-start.1 = (f32[32]{0:T(128)S(1)}, f32[32]{0:T(128)}, u32[]{:S(2)}) copy-start(f32[32]{0:T(128)} %param.8) | copy-start | bytes 388
  19.0 40.9 %all-to-all-start.1 = ((f32[16,1,4096]{2,1,0:T(1,128)}), f32[16,1,4096]{2,1,0:T(1,128)S(1)}, u32[]{:S(2)}, u32[]{:S(2)}) async-start(f32[16,1,4096]{2,1,0:T(1,128)} %reshape.76), calls=%async_computation.1 | async-start | bytes 524288 | tf_op jit(solution)/shard_map/all_to_all | solution.py:28
  59.9 16.2 %all-to-all-start = ((f32[16,1,4096]{2,1,0:T(1,128)}), f32[16,1,4096]{2,1,0:T(1,128)S(1)}, u32[]{:S(2)}, u32[]{:S(2)}) async-start(f32[16,1,4096]{2,1,0:T(1,128)} %reshape.74), calls=%async_computation | async-start | bytes 524288 | tf_op jit(solution)/shard_map/all_to_all | solution.py:27
  85.9 12.8 %all-to-all-start.3 = ((f32[16,32,128]{2,1,0:T(8,128)}), f32[16,32,128]{2,1,0:T(8,128)S(1)}, u32[]{:S(2)}, u32[]{:S(2)}) async-start(f32[16,32,128]{2,1,0:T(8,128)} %concatenate.31.clone), calls=%async_computation.3 | async-start | bytes 524288 | tf_op jit(solution)/shard_map/all_to_all | solution.py:34
  98.7 12.7 %all-to-all-start.2 = ((f32[16,32,128]{2,1,0:T(8,128)}), f32[16,32,128]{2,1,0:T(8,128)S(1)}, u32[]{:S(2)}, u32[]{:S(2)}) async-start(f32[16,32,128]{2,1,0:T(8,128)} %concatenate.29.clone), calls=%async_computation.2 | async-start | bytes 524288 | tf_op jit(solution)/shard_map/all_to_all | solution.py:33
where the time goes:
time: 192 us; the launch traced here: 191 us
  blocking collectives  78 us (41%)
  other arithmetic  28.9 us (15%)
  starting transfers between devices  22.3 us (12%)
  waiting for transfers between devices  22.1 us (12%)
  matrix products  21.8 us (11%)
  local copies, waits for them, and re-layouts  16.5 us (9%)
    psum x1, blocking collectives, body(): image = lax.psum(slab_colour_rgb, 'depth')  74.4 us
    dot_general x1, matrix products, body(): jnp.einsum('ij,jbr->ibr', lower, tau, precision=lax.Precision.HIGHEST)  21.2 us
    unnamed x2, other arithmetic  18.9 us
    all_to_all x1, waiting for transfers between devices, body(): lax.all_to_all(lead_light, 'depth', split_axis=0, concat_axis=2, tiled=True)  8.99 us
    all_to_all x1, starting transfers between devices, body(): lax.all_to_all(trans[None], 'depth', split_axis=2, concat_axis=0, tiled=T...  8.35 us
    all_to_all x1, waiting for transfers between devices, body(): lax.all_to_all(lead_trans, 'depth', split_axis=0, concat_axis=2, tiled=True)  7.84 us
    unnamed x14, local copies, waits for them, and re-layouts  7.74 us
    all_to_all x1, starting transfers between devices, body(): lax.all_to_all(light[None], 'depth', split_axis=2, concat_axis=0, tiled=T...  6.9 us
  transfers between devices with their start and end apart: 4, of which 3 were waited for; matrix products, arithmetic and copies ran while one was open for 20% of the time, Pallas kernels for 0%

commit v1 on v0

--- a/solution.py
+++ b/solution.py
@@ -31,7 +31,12 @@
     lead_light = jnp.concatenate([jnp.zeros_like(pieces[0][:1]), totals[0][:-1]], axis=0)
     lead_trans = jnp.concatenate([jnp.ones_like(pieces[1][:1]), totals[1][:-1]], axis=0)
     moved_light = lax.all_to_all(lead_light, "depth", split_axis=0, concat_axis=2, tiled=True)
-    moved_trans = lax.all_to_all(lead_trans, "depth", split_axis=0, concat_axis=2, tiled=True)
+    moved_trans = jnp.concatenate(
+        lax.all_to_all(
+            jnp.stack(jnp.split(lead_trans, lax.axis_size("depth"), axis=0)), "depth", 0, 0
+        ),
+        axis=2,
+    )
     nearer_radiance = moved_light[0]
     nearer_transparency = moved_trans[0]
     front_part = jnp.dot(response, nearer_radiance, precision=lax.Precision.HIGHEST)

time: 192 us -> 202 us (1.052)
  local copies, waits for them, and re-layouts: 16.5 us -> 25.7 us
    unnamed x14 -> x29, local copies, waits for them, and re-layouts: 7.74 us -> 16.9 us
    all_to_all x1, waiting for transfers between devices: 5.3 us -> 0.01 us  [body(): lax.all_to_all(light[None], 'depth', split_axis=2, concat_axis=0, tiled=T...]
    all_to_all x1, waiting for transfers between devices: 0.01 us -> 5.06 us  [body(): lax.all_to_all(trans[None], 'depth', split_axis=2, concat_axis=0, tiled=T...]
  transfers between devices with their start and end apart: 4 -> 4, of which waited for: 3 -> 3; matrix products, arithmetic and copies ran while one was open for 20% -> 11% of each run, Pallas kernels for 0% -> 0%
where the time goes in v1:
time: 202 us; the launch traced here: 201 us
  blocking collectives  78 us (39%)
  other arithmetic  29.1 us (14%)
  local copies, waits for them, and re-layouts  25.7 us (13%)
  matrix products  22.6 us (11%)
  starting transfers between devices  22.4 us (11%)
  waiting for transfers between devices  21.9 us (11%)
    psum x1, blocking collectives, body(): image = lax.psum(slab_colour_rgb, 'depth')  74.4 us
    dot_general x1, matrix products, body(): jnp.einsum('ij,jbr->ibr', lower, tau, precision=lax.Precision.HIGHEST)  21.9 us
    unnamed x2, other arithmetic  18.9 us
    unnamed x29, local copies, waits for them, and re-layouts  16.9 us
    all_to_all x1, waiting for transfers between devices, body(): lax.all_to_all(lead_light, 'depth', split_axis=0, concat_axis=2, tiled=True)  8.98 us
    all_to_all x1, starting transfers between devices, body(): lax.all_to_all(light[None], 'depth', split_axis=2, concat_axis=0, tiled=T...  8.34 us
    all_to_all x1, waiting for transfers between devices, body(): lax.all_to_all(jnp.stack(jnp.split(lead_trans, lax.axis_size('depth'), ax...  7.82 us
    all_to_all x1, starting transfers between devices, body(): lax.all_to_all(trans[None], 'depth', split_axis=2, concat_axis=0, tiled=T...  6.91 us
  transfers between devices with their start and end apart: 4, of which 3 were waited for; matrix products, arithmetic and copies ran while one was open for 11% of the time, Pallas kernels for 0%

profile of v1, /device:TPU:0, one launch (start us, length us, event | category | flops | bytes accessed | tf_op | source)
XLA Modules:
  0.0 200.9 jit_solution(1493234309250570717)
XLA Ops:
  0.7 0.8 and_select_fusion
  1.5 21.9 %multiply_reduce_fusion = f32[32,2048]{1,0:T(8,128)S(1)} fusion(bf16[32,32,2048]{2,1,0:T(8,128)(2,1)} %param.6, f32[32]{0:T(128)} %param.8, f32[32,2048]{1,0:T(8,128)S(1)} %and_select_fusion, bf16[32,32,2048]{2,1,0:T(8,128)(2,1)} %param.7), kind=kOutput, calls=%fused_computation | convolution fusion | flops 826214400 | bytes 8913024 | tf_op jit(solution)/shard_map/ij,jbr->ibr/dot_general | solution.py:21
  23.4 0.6 copy.118
  24.0 0.5 broadcast.86
  24.6 9.5 %reduce.2 = f32[2048,32]{1,0:T(8,128)S(1)} reduce(f32[2048,1,32]{2,1,0:T(1,128)S(1)} %bitcast.104, f32[]{:T(128)} %broadcast.86), dimensions={1}, to_apply=%bitcast.86.reduce_sub_computation | reduce | bytes 524292
  34.1 1.2 reshape.77
  35.2 8.3 %all-to-all-start = ((f32[16,1,4096]{2,1,0:T(1,128)}), f32[16,1,4096]{2,1,0:T(1,128)S(1)}, u32[]{:S(2)}, u32[]{:S(2)}) async-start(f32[16,1,4096]{2,1,0:T(1,128)} %reshape.77), calls=%async_computation | async-start | bytes 524288 | tf_op jit(solution)/shard_map/all_to_all | solution.py:27
  43.6 5.9 %fusion = f32[32,2048]{1,0:T(8,128)S(1)} fusion(f32[32]{0:T(128)S(1)} %copy-done.1, f32[32,2048]{1,0:T(8,128)S(1)} %and_select_fusion, bf16[32,32,2048]{2,1,0:T(8,128)(2,1)} %param.7), kind=kLoop, calls=%fused_computation.2 | loop fusion | flops 10420224 | bytes 4718720 | tf_op jit(solution)/shard_map/reduce_sum | solution.py:25
  49.5 0.6 copy.120
  50.1 9.3 %reduce = f32[2048,32]{1,0:T(8,128)S(1)} reduce(f32[2048,1,32]{2,1,0:T(1,128)S(1)} %bitcast.105, f32[]{:T(128)} %broadcast.86), dimensions={1}, to_apply=%bitcast.88.reduce_sub_computation | reduce | bytes 524292
  59.5 1.1 reshape.79
  60.6 6.9 %all-to-all-start.1 = ((f32[16,1,4096]{2,1,0:T(1,128)}), f32[16,1,4096]{2,1,0:T(1,128)S(1)}, u32[]{:S(2)}, u32[]{:S(2)}) async-start(f32[16,1,4096]{2,1,0:T(1,128)} %reshape.79), calls=%async_computation.1 | async-start | bytes 524288 | tf_op jit(solution)/shard_map/all_to_all | solution.py:28
  67.5 0.6 constant_dynamic-update-slice_fusion.15
  68.1 1.3 reduce.3
  69.4 1.8 reshape.78
  71.2 0.3 copy.142
  71.8 5.1 %all-to-all-done.1 = f32[16,1,4096]{2,1,0:T(1,128)S(1)} async-done(((f32[16,1,4096]{2,1,0:T(1,128)}), f32[16,1,4096]{2,1,0:T(1,128)S(1)}, u32[]{:S(2)}, u32[]{:S(2)}) %all-to-all-start.1) | async-done | bytes 262176 | tf_op jit(solution)/shard_map/all_to_all | solution.py:28
  76.8 1.3 reduce.1
  78.1 1.8 reshape.80
  79.9 0.6 copy.121
  82.5 0.4 pad.55
  83.0 0.4 pad.56
  83.4 0.4 pad.58
  83.8 0.4 pad.57
  86.9 0.6 constant_dynamic-update-slice_fusion.14
  87.5 0.6 constant_dynamic-update-slice_fusion.13
  88.1 0.6 constant_dynamic-update-slice_fusion.12
  88.7 0.6 constant_dynamic-update-slice_fusion.11
  89.3 0.6 constant_dynamic-update-slice_fusion.10
  89.9 0.6 constant_dynamic-update-slice_fusion.9
  90.5 0.6 constant_dynamic-update-slice_fusion.8
  91.1 0.6 constant_dynamic-update-slice_fusion.7
  91.7 0.6 constant_dynamic-update-slice_fusion.6
  92.3 0.6 constant_dynamic-update-slice_fusion.5
  92.9 0.6 constant_dynamic-update-slice_fusion.4
  93.5 0.6 constant_dynamic-update-slice_fusion.3
  94.1 0.6 constant_dynamic-update-slice_fusion.2
  94.7 0.6 constant_dynamic-update-slice_fusion.1
  95.3 0.6 constant_dynamic-update-slice_fusion
  95.9 3.5 %all-to-all-start.3 = ((f32[16,1,32,128]{3,2,1,0:T(8,128)}), f32[16,1,32,128]{3,2,1,0:T(8,128)S(1)}, u32[]{:S(2)}, u32[]{:S(2)}) async-start(f32[16,1,32,128]{3,2,1,0:T(8,128)} %constant_dynamic-update-slice_fusion), calls=%async_computation.3 | async-start | bytes 524288 | tf_op jit(solution)/shard_map/all_to_all | solution.py:35
  100.2 0.7 concatenate.26.clone
  100.9 7.8 %all-to-all-done.3 = f32[16,1,32,128]{3,2,1,0:T(8,128)S(1)} async-done(((f32[16,1,32,128]{3,2,1,0:T(8,128)}), f32[16,1,32,128]{3,2,1,0:T(8,128)S(1)}, u32[]{:S(2)}, u32[]{:S(2)}) %all-to-all-start.3) | async-done | bytes 262176 | tf_op jit(solution)/shard_map/all_to_all | solution.py:35
  108.7 3.5 %all-to-all-start.2 = ((f32[16,32,128]{2,1,0:T(8,128)}), f32[16,32,128]{2,1,0:T(8,128)S(1)}, u32[]{:S(2)}, u32[]{:S(2)}) async-start(f32[16,32,128]{2,1,0:T(8,128)} %concatenate.26.clone), calls=%async_computation.2 | async-start | bytes 524288 | tf_op jit(solution)/shard_map/all_to_all | solution.py:33
  112.4 9.0 %all-to-all-done.2 = f32[16,32,128]{2,1,0:T(8,128)S(1)} async-done(((f32[16,32,128]{2,1,0:T(8,128)}), f32[16,32,128]{2,1,0:T(8,128)S(1)}, u32[]{:S(2)}, u32[]{:S(2)}) %all-to-all-start.2) | async-done | bytes 262176 | tf_op jit(solution)/shard_map/all_to_all | solution.py:33
  121.6 0.3 convolution_bitcast_fusion
  122.2 3.6 %all-reduce.17 = (f32[1,3,2048]{2,1,0:T(4,128)S(1)}, f32[3,2048]{1,0:T(4,128)S(1)}) all-reduce(f32[1,3,2048]{2,1,0:T(4,128)S(1)} %convolution_bitcast_fusion.1, f32[3,2048]{1,0:T(4,128)S(1)} %convolution_bitcast_fusion), channel_id=1, replica_groups=mesh['depth'=16,'spec'=2] {'spec'}, use_global_device_ids=true, to_apply=%region_2.3 | all-reduce | flops 12288 | bytes 98304 | tf_op jit(solution)/shard_map/psum | solution.py:44
  125.9 74.4 %psum.23 = f32[3,2048]{1,0:T(4,128)} all-reduce(f32[3,2048]{1,0:T(4,128)S(1)} %get-tuple-element.15), channel_id=1, replica_groups=mesh['depth'=16,'spec'=2] {'depth'}, use_global_device_ids=true, to_apply=%region_4.5 | all-reduce | flops 6144 | bytes 49152 | tf_op jit(solution)/shard_map/psum | solution.py:45
  200.2 0.6 copy.141
  (63 shorter events, 5.9 us)
Async XLA Ops:
  0.6 120.9 %copy-start = (f32[3,32]{1,0:T(4,128)S(1)}, f32[3,32]{1,0:T(4,128)}, u32[]{:S(2)}) copy-start(f32[3,32]{1,0:T(4,128)} %param.11) | copy-start | bytes 1156
  23.4 20.2 %copy-start.1 = (f32[32]{0:T(128)S(1)}, f32[32]{0:T(128)}, u32[]{:S(2)}) copy-start(f32[32]{0:T(128)} %param.8) | copy-start | bytes 388
  35.2 25.4 %all-to-all-start = ((f32[16,1,4096]{2,1,0:T(1,128)}), f32[16,1,4096]{2,1,0:T(1,128)S(1)}, u32[]{:S(2)}, u32[]{:S(2)}) async-start(f32[16,1,4096]{2,1,0:T(1,128)} %reshape.77), calls=%async_computation | async-start | bytes 524288 | tf_op jit(solution)/shard_map/all_to_all | solution.py:27
  60.6 16.2 %all-to-all-start.1 = ((f32[16,1,4096]{2,1,0:T(1,128)}), f32[16,1,4096]{2,1,0:T(1,128)S(1)}, u32[]{:S(2)}, u32[]{:S(2)}) async-start(f32[16,1,4096]{2,1,0:T(1,128)} %reshape.79), calls=%async_computation.1 | async-start | bytes 524288 | tf_op jit(solution)/shard_map/all_to_all | solution.py:28
  95.9 12.8 %all-to-all-start.3 = ((f32[16,1,32,128]{3,2,1,0:T(8,128)}), f32[16,1,32,128]{3,2,1,0:T(8,128)S(1)}, u32[]{:S(2)}, u32[]{:S(2)}) async-start(f32[16,1,32,128]{3,2,1,0:T(8,128)} %constant_dynamic-update-slice_fusion), calls=%async_computation.3 | async-start | bytes 524288 | tf_op jit(solution)/shard_map/all_to_all | solution.py:35
  108.7 12.7 %all-to-all-start.2 = ((f32[16,32,128]{2,1,0:T(8,128)}), f32[16,32,128]{2,1,0:T(8,128)S(1)}, u32[]{:S(2)}, u32[]{:S(2)}) async-start(f32[16,32,128]{2,1,0:T(8,128)} %concatenate.26.clone), calls=%async_computation.2 | async-start | bytes 524288 | tf_op jit(solution)/shard_map/all_to_all | solution.py:33
